TPU v7x, 512 devices: a whole 4x4x16 slice. The times are simulated.
512 devices in a mesh: row: 64 (over z, x), col: 8 (over y, core).
Axes of the slice: x: 4, y: 4, z: 16, core: 2. Of those that a mesh axis runs over, the one named last changes fastest.
Arguments:
- gate_up: bfloat16 [4, 2, 14336, 4096], P(None, None, 'row', 'col'), may hold values from -0.09375 to 0.09375
- down_weight: bfloat16 [4, 4096, 14336], P(None, 'row', 'col'), may hold values from -0.046875 to 0.046875
- query_output: bfloat16 [4, 2, 4096, 4096], P(None, None, 'row', 'col'), may hold values from -0.09375 to 0.09375
- probe_gate: bfloat16 [4, 2, 16, 4096], P(None, None, None, 'col'), may hold values from -6 to 6
- probe_down: bfloat16 [4, 16, 14336], P(None, None, 'col'), may hold values from -6 to 6
- probe_query: bfloat16 [4, 2, 16, 4096], P(None, None, None, 'col'), may hold values from -6 to 6
Outputs:
- vector_gate: float32 [4, 2, 16, 4096], P(None, None, None, 'col')
- vector_down: float32 [4, 16, 14336], P(None, None, 'col')
- vector_query: float32 [4, 2, 16, 4096], P(None, None, None, 'col')
- sigma_gate: float32 [4, 2, 16], replicated
- sigma_down: float32 [4, 16], replicated
- sigma_query: float32 [4, 2, 16], replicated
All inputs are finite; a program needn't handle non-finite values.
Results may differ from a plain program's by a relative error of at most 0.0033.
Values may be sent and summed in bfloat16 or wider, within the bound.
No kernel may reach another device: no remote copies, remote signals or barrier semaphores. Data moves between devices by JAX's collectives and lax.ppermute only.
A program may use at most 64 MiB of HBM per device.

v0:
```python
import jax
import jax.numpy as jnp
from jax import lax
from jax.sharding import Mesh
from jax.sharding import PartitionSpec as P

ITERS = 2
ROW = ("row_0", "row_1")
epsilon = 1e-06


def copy_for_each(shard, axis):
    length = lax.axis_size(axis)
    return lax.all_to_all(
        jnp.broadcast_to(shard[None], (length, *shard.shape)), axis, 0, 0, tiled=True
    )


def of_everyone(shard, axis):
    everything = copy_for_each(shard, axis)
    return jnp.sum(everything, axis=0)


def over_axes(shard, axes):
    for axis in axes:
        shard = lax.psum(shard, axis)
    return shard


def body(gate_up, down_weight, query_output, probe_gate, probe_down, probe_query):
    row_count = lax.axis_size(ROW)
    col_count = lax.axis_size("col")
    weights = (gate_up, down_weight[:, None], query_output)
    vectors = (probe_gate, probe_down[:, None], probe_query)
    scaled_right = vectors
    spectral = None

    def left_factor(total, weight):
        return lax.rsqrt(total[..., None] / (weight.shape[2] * row_count) + epsilon)

    for turn in range(ITERS):
        partial_value = tuple(
            (
                jnp.einsum("lmoi,lmki->lmko", weight, vector, preferred_element_type=jnp.float32)
                for weight, vector in zip(weights, vectors)
            )
        )
        summed = jax.tree.map(lambda part: of_everyone(part, "col"), partial_value)
        squares = tuple((jnp.sum(piece * piece, axis=3) for piece in summed))
        totals = jax.tree.map(lambda part: over_axes(part, ROW), squares)
        left_vecs = tuple((piece.astype(jnp.bfloat16) for piece in summed))
        right_partial = tuple(
            (
                jnp.einsum("lmoi,lmko->lmki", weight, left, preferred_element_type=jnp.float32)
                for weight, left in zip(weights, left_vecs)
            )
        )
        raw_sums = lax.psum(right_partial, ROW)
        right_sums = tuple(
            (
                raw * left_factor(total, weight)
                for raw, total, weight in zip(raw_sums, totals, weights)
            )
        )
        right_squares = tuple((jnp.sum(piece * piece, axis=3) for piece in right_sums))
        right_totals = jax.tree.map(lambda part: of_everyone(part, "col"), right_squares)
        scaled_right = tuple(
            (
                piece * lax.rsqrt(total[..., None] / (piece.shape[3] * col_count) + epsilon)
                for piece, total in zip(right_sums, right_totals)
            )
        )
        spectral = tuple(
            (
                jnp.sqrt(total / (weight.shape[2] * row_count))
                for weight, total in zip(weights, right_totals)
            )
        )
        vectors = tuple((piece.astype(jnp.bfloat16) for piece in scaled_right))
    return (
        scaled_right[0],
        scaled_right[1][:, 0],
        scaled_right[2],
        spectral[0],
        spectral[1][:, 0],
        spectral[2],
    )


def solution(mesh):
    finer = Mesh(mesh.devices.reshape(16, 4, mesh.shape["col"]), ("row_0", "row_1", "col"))
    in_specs = (
        P(None, None, ROW, "col"),
        P(None, ROW, "col"),
        P(None, None, ROW, "col"),
        P(None, None, None, "col"),
        P(None, None, "col"),
        P(None, None, None, "col"),
    )
    out_specs = (
        P(None, None, None, "col"),
        P(None, None, "col"),
        P(None, None, None, "col"),
        P(),
        P(),
        P(),
    )
    return jax.shard_map(body, mesh=finer, in_specs=in_specs, out_specs=out_specs, check_vma=False)
```

profile of v0, /device:TPU:1, one launch (start us, length us, event | category | flops | bytes accessed | tf_op | source)
XLA Modules:
  0.0 717.1 jit_solution(13803138326627123436)
XLA Ops:
  9.9 10.1 %all-to-all-start.4 = ((f32[8,1,4096]{2,1,0:T(1,128)}), f32[8,1,4096]{2,1,0:T(1,128)S(1)}, u32[]{:S(2)}, u32[]{:S(2)}) async-start(f32[8,1,4096]{2,1,0:T(1,128)} %reshape.197), calls=%async_computation.4 | async-start | bytes 262144 | tf_op jit(solution)/shard_map/all_to_all | solution.py:14
  21.3 3.9 all-to-all-done.4
  25.2 4.2 all-to-all-start.8
  30.7 5.2 all-to-all-done.8
  38.1 5.1 all-to-all-start
  61.1 45.7 %all-reduce.3 = (f32[4,2,16]{2,1,0:T(2,128)S(1)}, f32[4,1,16]{2,0,1:T(4,128)S(1)}, f32[4,2,16]{2,1,0:T(2,128)S(1)}) all-reduce(f32[4,2,16]{2,1,0:T(2,128)S(1)} %multiply_reduce_fusion.7, f32[4,1,16]{2,0,1:T(4,128)S(1)} %bitcast.30, f32[4,2,16]{2,1,0:T(2,128)S(1)} %multiply_reduce_fusion.9), channel_id=1, replica_groups=mesh['row_0'=16,'row_1'=4,'col'=8] {'row_0'}, use_global_device_ids=true, to_apply=%region_3.0 | all-reduce | flops 320 | bytes 2560 | tf_op jit(solution)/shard_map/psum | solution.py:26
  106.7 13.6 %all-reduce.5 = (f32[4,2,16]{2,1,0:T(2,128)S(1)}, f32[4,1,16]{2,0,1:T(4,128)S(1)}, f32[4,2,16]{2,1,0:T(2,128)S(1)}) all-reduce(f32[4,2,16]{2,1,0:T(2,128)S(1)} %get-tuple-element.15, f32[4,1,16]{2,0,1:T(4,128)S(1)} %get-tuple-element.16, f32[4,2,16]{2,1,0:T(2,128)S(1)} %get-tuple-element.17), channel_id=1, replica_groups=mesh['row_0'=16,'row_1'=4,'col'=8] {'row_1'}, use_global_device_ids=true, to_apply=%region_4.0 | all-reduce | flops 320 | bytes 2560 | tf_op jit(solution)/shard_map/psum | solution.py:26
  120.3 203.2 %all-reduce.11.cloned.1.call-done = (f32[4,2,16,512]{3,2,1,0:T(8,128)}, f32[4,1,16,1792]{3,2,0,1:T(8,128)}, f32[4,2,16,512]{3,2,1,0:T(8,128)}) async-done(((f32[4,2,16,512]{3,2,1,0:T(8,128)}, f32[4,1,16,1792]{3,2,0,1:T(8,128)}, f32[4,2,16,512]{3,2,1,0:T(8,128)}), (f32[4,2,16,512]{3,2,1,0:T(8,128)}, f32[4,1,16,1792]{3,2,0,1:T(8,128)}, f32[4,2,16,512]{3,2,1,0:T(8,128)})) %all-reduce.11.cloned.1.call-update) | async-done | bytes 983056 | tf_op jit(solution)/shard_map/psum | solution.py:58
  325.4 15.1 %all-to-all-start.5 = ((f32[8,4,1,16]{3,2,1,0:T(1,128)}), f32[8,4,1,16]{3,2,1,0:T(1,128)S(1)}, u32[]{:S(2)}, u32[]{:S(2)}) async-start(f32[8,4,1,16]{3,2,1,0:T(1,128)} %broadcast_in_dim.29), calls=%async_computation.5 | async-start | bytes 32768 | tf_op jit(solution)/shard_map/all_to_all | solution.py:14
  345.1 3.9 all-to-all-start.9
  354.2 4.3 all-to-all-start.1
  365.5 4.8 all-to-all-start.6
  372.4 3.3 all-to-all-done.6
  375.6 4.8 all-to-all-start.10
  381.7 5.3 all-to-all-done.10
  389.1 5.1 all-to-all-start.2
  394.2 2.4 reduce.13
  403.4 6.0 all-to-all-done.2
  412.1 41.4 %all-reduce.2 = (f32[4,2,16]{2,1,0:T(2,128)S(1)}, f32[4,1,16]{2,0,1:T(4,128)S(1)}, f32[4,2,16]{2,1,0:T(2,128)S(1)}) all-reduce(f32[4,2,16]{2,1,0:T(2,128)S(1)} %multiply_reduce_fusion.6, f32[4,1,16]{2,0,1:T(4,128)S(1)} %bitcast.31, f32[4,2,16]{2,1,0:T(2,128)S(1)} %multiply_reduce_fusion.8), channel_id=1, replica_groups=mesh['row_0'=16,'row_1'=4,'col'=8] {'row_0'}, use_global_device_ids=true, to_apply=%region_10.0 | all-reduce | flops 320 | bytes 2560 | tf_op jit(solution)/shard_map/psum | solution.py:26
  453.4 13.0 %all-reduce.4 = (f32[4,2,16]{2,1,0:T(2,128)S(1)}, f32[4,1,16]{2,0,1:T(4,128)S(1)}, f32[4,2,16]{2,1,0:T(2,128)S(1)}) all-reduce(f32[4,2,16]{2,1,0:T(2,128)S(1)} %get-tuple-element.12, f32[4,1,16]{2,0,1:T(4,128)S(1)} %get-tuple-element.13, f32[4,2,16]{2,1,0:T(2,128)S(1)} %get-tuple-element.14), channel_id=1, replica_groups=mesh['row_0'=16,'row_1'=4,'col'=8] {'row_1'}, use_global_device_ids=true, to_apply=%region_11.0 | all-reduce | flops 320 | bytes 2560 | tf_op jit(solution)/shard_map/psum | solution.py:26
  466.4 203.1 %all-reduce.9.cloned.1.call-done = (f32[4,2,16,512]{3,2,1,0:T(8,128)}, f32[4,1,16,1792]{3,2,0,1:T(8,128)}, f32[4,2,16,512]{3,2,1,0:T(8,128)}) async-done(((f32[4,2,16,512]{3,2,1,0:T(8,128)}, f32[4,1,16,1792]{3,2,0,1:T(8,128)}, f32[4,2,16,512]{3,2,1,0:T(8,128)}), (f32[4,2,16,512]{3,2,1,0:T(8,128)}, f32[4,1,16,1792]{3,2,0,1:T(8,128)}, f32[4,2,16,512]{3,2,1,0:T(8,128)})) %all-reduce.9.cloned.1.call-update) | async-done | bytes 983056 | tf_op jit(solution)/shard_map/psum | solution.py:58
  671.5 15.1 %all-to-all-start.7 = ((f32[8,4,1,16]{3,2,1,0:T(1,128)}), f32[8,4,1,16]{3,2,1,0:T(1,128)S(1)}, u32[]{:S(2)}, u32[]{:S(2)}) async-start(f32[8,4,1,16]{3,2,1,0:T(1,128)} %broadcast_in_dim.31), calls=%async_computation.7 | async-start | bytes 32768 | tf_op jit(solution)/shard_map/all_to_all | solution.py:14
  691.2 3.9 all-to-all-start.11
  699.7 3.9 all-to-all-start.3
  (123 shorter events, 76.3 us)
Async XLA Ops:
  7.2 22.3 %copy-start = (bf16[4,2,224,512]{3,2,1,0:T(8,128)(2,1)S(1)}, bf16[4,2,224,512]{3,2,1,0:T(8,128)(2,1)}, u32[]{:S(2)}) copy-start(bf16[4,2,224,512]{3,2,1,0:T(8,128)(2,1)} %param.6) | copy-start | bytes 5505028
  7.2 12.8 %copy-start.11 = (bf16[4,2,16,512]{3,2,1,0:T(8,128)(2,1)S(1)}, bf16[4,2,16,512]{3,2,1,0:T(8,128)(2,1)}, u32[]{:S(2)}) copy-start(bf16[4,2,16,512]{3,2,1,0:T(8,128)(2,1)} %param.11) | copy-start | bytes 393220
  7.2 12.8 %copy-start.2 = (bf16[4,2,64,512]{3,2,1,0:T(8,128)(2,1)S(1)}, bf16[4,2,64,512]{3,2,1,0:T(8,128)(2,1)}, u32[]{:S(2)}) copy-start(bf16[4,2,64,512]{3,2,1,0:T(8,128)(2,1)} %param.8) | copy-start | bytes 1572868
  9.0 20.4 %copy-start.10 = (bf16[4,2,16,512]{3,2,1,0:T(8,128)(2,1)S(1)}, bf16[4,2,16,512]{3,2,1,0:T(8,128)(2,1)}, u32[]{:S(2)}) copy-start(bf16[4,2,16,512]{3,2,1,0:T(8,128)(2,1)} %param.9) | copy-start | bytes 393220
  9.9 15.4 %all-to-all-start.4 = ((f32[8,1,4096]{2,1,0:T(1,128)}), f32[8,1,4096]{2,1,0:T(1,128)S(1)}, u32[]{:S(2)}, u32[]{:S(2)}) async-start(f32[8,1,4096]{2,1,0:T(1,128)} %reshape.197), calls=%async_computation.4 | async-start | bytes 262144 | tf_op jit(solution)/shard_map/all_to_all | solution.py:14
  25.2 4.2 copy-start.7
  25.2 10.7 %all-to-all-start.8 = ((f32[8,1,8192]{2,1,0:T(1,128)}), f32[8,1,8192]{2,1,0:T(1,128)S(1)}, u32[]{:S(2)}, u32[]{:S(2)}) async-start(f32[8,1,8192]{2,1,0:T(1,128)} %reshape.201), calls=%async_computation.8 | async-start | bytes 524288 | tf_op jit(solution)/shard_map/all_to_all | solution.py:14
  30.7 18.8 %copy-start.1 = (bf16[4,64,1792]{2,1,0:T(8,128)(2,1)S(1)}, bf16[4,64,1792]{2,1,0:T(8,128)(2,1)}, u32[]{:S(2)}) copy-start(bf16[4,64,1792]{2,1,0:T(8,128)(2,1)} %param.7) | copy-start | bytes 2752516
  35.9 12.0 %copy-start.4 = (f32[8,1,8192]{2,1,0:T(1,128)}, f32[8,1,8192]{2,1,0:T(1,128)S(1)}, u32[]{:S(2)}) copy-start(f32[8,1,8192]{2,1,0:T(1,128)S(1)} %all-to-all-done.8) | copy-start | bytes 786436
  38.1 20.2 %all-to-all-start = ((f32[8,4,2,16,224]{4,3,2,1,0:T(8,128)}), f32[8,4,2,16,224]{4,3,2,1,0:T(8,128)}, u32[]{:S(2)}, u32[]{:S(2)}) async-start(f32[8,4,2,16,224]{4,3,2,1,0:T(8,128)} %broadcast_in_dim.24), calls=%async_computation | async-start | bytes 2097152 | tf_op jit(solution)/shard_map/all_to_all | solution.py:14
  43.2 280.4 %all-reduce.11.cloned.1.call-start = ((), (), s32[]{:S(2)}) async-start(), calls=%async_computation.13 | async-start | bytes 1966080 | tf_op jit(solution)/shard_map/psum | solution.py:58
  325.4 19.7 %all-to-all-start.5 = ((f32[8,4,1,16]{3,2,1,0:T(1,128)}), f32[8,4,1,16]{3,2,1,0:T(1,128)S(1)}, u32[]{:S(2)}, u32[]{:S(2)}) async-start(f32[8,4,1,16]{3,2,1,0:T(1,128)} %broadcast_in_dim.29), calls=%async_computation.5 | async-start | bytes 32768 | tf_op jit(solution)/shard_map/all_to_all | solution.py:14
  345.1 8.5 %all-to-all-start.9 = ((f32[8,1,128]{2,1,0:T(1,128)}), f32[8,1,128]{2,1,0:T(1,128)S(1)}, u32[]{:S(2)}, u32[]{:S(2)}) async-start(f32[8,1,128]{2,1,0:T(1,128)} %reshape.203), calls=%async_computation.9 | async-start | bytes 8192 | tf_op jit(solution)/shard_map/all_to_all | solution.py:14
  351.3 29.1 %copy-start.3 = (f32[4,2,16,512]{3,2,1,0:T(8,128)S(1)}, f32[4,2,16,512]{3,2,1,0:T(8,128)}, u32[]{:S(2)}) copy-start(f32[4,2,16,512]{3,2,1,0:T(8,128)} %get-tuple-element.9) | copy-start | bytes 786436
  354.2 11.3 %all-to-all-start.1 = ((f32[8,1,128]{2,1,0:T(1,128)}), f32[8,1,128]{2,1,0:T(1,128)S(1)}, u32[]{:S(2)}, u32[]{:S(2)}) async-start(f32[8,1,128]{2,1,0:T(1,128)} %reshape.193), calls=%async_computation.1 | async-start | bytes 8192 | tf_op jit(solution)/shard_map/all_to_all | solution.py:14
  365.5 10.2 %all-to-all-start.6 = ((f32[8,1,4096]{2,1,0:T(1,128)}), f32[8,1,4096]{2,1,0:T(1,128)}, u32[]{:S(2)}, u32[]{:S(2)}) async-start(f32[8,1,4096]{2,1,0:T(1,128)} %reshape.199), calls=%async_computation.6 | async-start | bytes 262144 | tf_op jit(solution)/shard_map/all_to_all | solution.py:14
  375.6 11.4 %all-to-all-start.10 = ((f32[8,1,8192]{2,1,0:T(1,128)}), f32[8,1,8192]{2,1,0:T(1,128)}, u32[]{:S(2)}, u32[]{:S(2)}) async-start(f32[8,1,8192]{2,1,0:T(1,128)} %reshape.205), calls=%async_computation.10 | async-start | bytes 524288 | tf_op jit(solution)/shard_map/all_to_all | solution.py:14
  389.1 20.2 %all-to-all-start.2 = ((f32[8,4,2,16,224]{4,3,2,1,0:T(8,128)}), f32[8,4,2,16,224]{4,3,2,1,0:T(8,128)}, u32[]{:S(2)}, u32[]{:S(2)}) async-start(f32[8,4,2,16,224]{4,3,2,1,0:T(8,128)} %broadcast_in_dim.26), calls=%async_computation.2 | async-start | bytes 2097152 | tf_op jit(solution)/shard_map/all_to_all | solution.py:14
  394.2 275.3 %all-reduce.9.cloned.1.call-start = ((), (), s32[]{:S(2)}) async-start(), calls=%async_computation.12 | async-start | bytes 1966080 | tf_op jit(solution)/shard_map/psum | solution.py:58
  669.6 35.3 %copy-start.6 = (f32[4,2,16,512]{3,2,1,0:T(8,128)S(1)}, f32[4,2,16,512]{3,2,1,0:T(8,128)}, u32[]{:S(2)}) copy-start(f32[4,2,16,512]{3,2,1,0:T(8,128)} %get-tuple-element.8) | copy-start | bytes 786436
  669.6 39.9 %copy-start.5 = (f32[4,2,16,512]{3,2,1,0:T(8,128)S(1)}, f32[4,2,16,512]{3,2,1,0:T(8,128)}, u32[]{:S(2)}) copy-start(f32[4,2,16,512]{3,2,1,0:T(8,128)} %get-tuple-element.6) | copy-start | bytes 786436
  671.5 19.7 %all-to-all-start.7 = ((f32[8,4,1,16]{3,2,1,0:T(1,128)}), f32[8,4,1,16]{3,2,1,0:T(1,128)S(1)}, u32[]{:S(2)}, u32[]{:S(2)}) async-start(f32[8,4,1,16]{3,2,1,0:T(1,128)} %broadcast_in_dim.31), calls=%async_computation.7 | async-start | bytes 32768 | tf_op jit(solution)/shard_map/all_to_all | solution.py:14
  691.2 8.5 %all-to-all-start.11 = ((f32[8,1,128]{2,1,0:T(1,128)}), f32[8,1,128]{2,1,0:T(1,128)S(1)}, u32[]{:S(2)}, u32[]{:S(2)}) async-start(f32[8,1,128]{2,1,0:T(1,128)} %reshape.207), calls=%async_computation.11 | async-start | bytes 8192 | tf_op jit(solution)/shard_map/all_to_all | solution.py:14
  699.7 8.5 %all-to-all-start.3 = ((f32[8,1,128]{2,1,0:T(1,128)}), f32[8,1,128]{2,1,0:T(1,128)S(1)}, u32[]{:S(2)}, u32[]{:S(2)}) async-start(f32[8,1,128]{2,1,0:T(1,128)} %reshape.195), calls=%async_computation.3 | async-start | bytes 8192 | tf_op jit(solution)/shard_map/all_to_all | solution.py:14
  (3 other events, 2.8 us)
Sparse Core Ops, SparseCore 0:
  60.9 262.6 all-reduce.10
  411.9 257.6 all-reduce.8
where the time goes:
time: 719 us; the launch traced here: 717 us
  waiting for transfers between devices  439 us (61%)
  blocking collectives  114 us (16%)
  starting transfers between devices  80.4 us (11%)
  other arithmetic  32.7 us (5%)
  local copies, waits for them, and re-layouts  22.5 us (3%)
  matrix products  14.6 us (2%)
  between operations  14.3 us (2%)
    psum x2, waiting for transfers between devices, body(): raw_sums = lax.psum(right_partial, ROW)  406 us
    psum x4, blocking collectives, over_axes(): shard = lax.psum(shard, axis)  114 us
    all_to_all x12, starting transfers between devices, copy_for_each(): lax.all_to_all(jnp.broadcast_to(shard[None], (length, *shard.shape)), axi...  80.4 us
    all_to_all x12, waiting for transfers between devices, copy_for_each(): lax.all_to_all(jnp.broadcast_to(shard[None], (length, *shard.shape)), axi...  32.5 us
    unnamed x42, local copies, waits for them, and re-layouts  14.8 us
  transfers between devices with their start and end apart: 14, of which 13 were waited for; matrix products, arithmetic and copies ran while one was open for 7% of the time, Pallas kernels for 0%

commit v1 on v0

--- a/solution.py
+++ b/solution.py
@@ -55,7 +55,7 @@
                 for weight, left in zip(weights, left_vecs)
             )
         )
-        raw_sums = lax.psum(right_partial, ROW)
+        raw_sums = lax.psum(lax.psum(right_partial, axis_name="row_0"), axis_name="row_1")
         right_sums = tuple(
             (
                 raw * left_factor(total, weight)

time: 719 us -> 592 us (0.82)
  waiting for transfers between devices: 439 us -> 308 us
  starting transfers between devices: 80.4 us -> 88.1 us
    psum x2 -> x4, waiting for transfers between devices: 406 us -> 275 us  [the longest x2 251 us: body(): lax.psum(right_partial, axis_name='row_0')]
    all_to_all x12, starting transfers between devices: 80.4 us -> 88 us  [copy_for_each(): lax.all_to_all(jnp.broadcast_to(shard[None], (length, *shard.shape)), axi...]
  transfers between devices with their start and end apart: 14 -> 16, of which waited for: 13 -> 15; matrix products, arithmetic and copies ran while one was open for 7% -> 9% of each run, Pallas kernels for 0% -> 0%
where the time goes in v1:
time: 592 us; the launch traced here: 590 us
  waiting for transfers between devices  308 us (52%)
  blocking collectives  110 us (19%)
  starting transfers between devices  88.1 us (15%)
  other arithmetic  32.7 us (6%)
  local copies, waits for them, and re-layouts  22.5 us (4%)
  matrix products  14.6 us (2%)
  between operations  14 us (2%)
    psum x2, waiting for transfers between devices, body(): lax.psum(right_partial, axis_name='row_0')  251 us
    psum x4, blocking collectives, over_axes(): shard = lax.psum(shard, axis)  110 us
    all_to_all x12, starting transfers between devices, copy_for_each(): lax.all_to_all(jnp.broadcast_to(shard[None], (length, *shard.shape)), axi...  88 us
    all_to_all x12, waiting for transfers between devices, copy_for_each(): lax.all_to_all(jnp.broadcast_to(shard[None], (length, *shard.shape)), axi...  32.5 us
    psum x2, waiting for transfers between devices, body(): lax.psum(lax.psum(right_partial, axis_name='row_0'), axis_name='row_1')  24 us
    unnamed x42, local copies, waits for them, and re-layouts  14.8 us
    all_to_all x8, other arithmetic, copy_for_each(): lax.all_to_all(jnp.broadcast_to(shard[None], (length, *shard.shape)), axi...  12.1 us
  transfers between devices with their start and end apart: 16, of which 15 were waited for; matrix products, arithmetic and copies ran while one was open for 9% of the time, Pallas kernels for 0%

profile of v1, /device:TPU:1, one launch (start us, length us, event | category | flops | bytes accessed | tf_op | source)
XLA Modules:
  0.0 590.1 jit_solution(188110429424923371)
XLA Ops:
  9.9 10.1 %all-to-all-start.4 = ((f32[8,1,4096]{2,1,0:T(1,128)}), f32[8,1,4096]{2,1,0:T(1,128)S(1)}, u32[]{:S(2)}, u32[]{:S(2)}) async-start(f32[8,1,4096]{2,1,0:T(1,128)} %reshape.197), calls=%async_computation.4 | async-start | bytes 262144 | tf_op jit(solution)/shard_map/all_to_all | solution.py:14
  21.3 3.9 all-to-all-done.4
  25.2 4.2 all-to-all-start.8
  30.7 5.2 all-to-all-done.8
  38.1 5.1 all-to-all-start
  60.8 128.9 %all-reduce.15.cloned.1.call-done = (f32[4,2,16,512]{3,2,1,0:T(8,128)}, f32[4,1,16,1792]{3,2,0,1:T(8,128)}, f32[4,2,16,512]{3,2,1,0:T(8,128)}) async-done(((f32[4,2,16,512]{3,2,1,0:T(8,128)}, f32[4,1,16,1792]{3,2,0,1:T(8,128)}, f32[4,2,16,512]{3,2,1,0:T(8,128)}), (f32[4,2,16,512]{3,2,1,0:T(8,128)}, f32[4,1,16,1792]{3,2,0,1:T(8,128)}, f32[4,2,16,512]{3,2,1,0:T(8,128)})) %all-reduce.15.cloned.1.call-update) | async-done | bytes 983056 | tf_op jit(solution)/shard_map/psum | solution.py:58
  190.1 41.3 %all-reduce.1 = (f32[4,2,16]{2,1,0:T(2,128)S(1)}, f32[4,1,16]{2,0,1:T(4,128)S(1)}, f32[4,2,16]{2,1,0:T(2,128)S(1)}) all-reduce(f32[4,2,16]{2,1,0:T(2,128)S(1)} %multiply_reduce_fusion.7, f32[4,1,16]{2,0,1:T(4,128)S(1)} %bitcast.30, f32[4,2,16]{2,1,0:T(2,128)S(1)} %multiply_reduce_fusion.9), channel_id=1, replica_groups=mesh['row_0'=16,'row_1'=4,'col'=8] {'row_0'}, use_global_device_ids=true, to_apply=%region_4.0 | all-reduce | flops 320 | bytes 2560 | tf_op jit(solution)/shard_map/psum | solution.py:26
  231.4 13.9 %all-reduce.5 = (f32[4,2,16]{2,1,0:T(2,128)S(1)}, f32[4,1,16]{2,0,1:T(4,128)S(1)}, f32[4,2,16]{2,1,0:T(2,128)S(1)}) all-reduce(f32[4,2,16]{2,1,0:T(2,128)S(1)} %get-tuple-element.9, f32[4,1,16]{2,0,1:T(4,128)S(1)} %get-tuple-element.10, f32[4,2,16]{2,1,0:T(2,128)S(1)} %get-tuple-element.11), channel_id=1, replica_groups=mesh['row_0'=16,'row_1'=4,'col'=8] {'row_1'}, use_global_device_ids=true, to_apply=%region_5.0 | all-reduce | flops 320 | bytes 2560 | tf_op jit(solution)/shard_map/psum | solution.py:26
  245.3 12.1 %all-reduce.19.cloned.1.call-done = (f32[4,2,16,512]{3,2,1,0:T(8,128)}, f32[4,1,16,1792]{3,2,0,1:T(8,128)}, f32[4,2,16,512]{3,2,1,0:T(8,128)}) async-done(((f32[4,2,16,512]{3,2,1,0:T(8,128)}, f32[4,1,16,1792]{3,2,0,1:T(8,128)}, f32[4,2,16,512]{3,2,1,0:T(8,128)}), (f32[4,2,16,512]{3,2,1,0:T(8,128)}, f32[4,1,16,1792]{3,2,0,1:T(8,128)}, f32[4,2,16,512]{3,2,1,0:T(8,128)})) %all-reduce.19.cloned.1.call-update) | async-done | bytes 983056 | tf_op jit(solution)/shard_map/psum | solution.py:58
  259.2 18.8 %all-to-all-start.5 = ((f32[8,4,1,16]{3,2,1,0:T(1,128)}), f32[8,4,1,16]{3,2,1,0:T(1,128)S(1)}, u32[]{:S(2)}, u32[]{:S(2)}) async-start(f32[8,4,1,16]{3,2,1,0:T(1,128)} %broadcast_in_dim.29), calls=%async_computation.5 | async-start | bytes 32768 | tf_op jit(solution)/shard_map/all_to_all | solution.py:14
  282.7 3.9 all-to-all-start.9
  291.7 4.3 all-to-all-start.1
  303.0 4.8 all-to-all-start.6
  313.2 4.8 all-to-all-start.10
  319.2 5.3 all-to-all-done.10
  326.6 5.1 all-to-all-start.2
  340.9 6.0 %all-to-all-done.2 = f32[8,4,2,16,224]{4,3,2,1,0:T(8,128)} async-done(((f32[8,4,2,16,224]{4,3,2,1,0:T(8,128)}), f32[8,4,2,16,224]{4,3,2,1,0:T(8,128)}, u32[]{:S(2)}, u32[]{:S(2)}) %all-to-all-start.2) | async-done | bytes 917536 | tf_op jit(solution)/shard_map/all_to_all | solution.py:14
  349.3 122.2 %all-reduce.13.cloned.1.call-done = (f32[4,2,16,512]{3,2,1,0:T(8,128)}, f32[4,1,16,1792]{3,2,0,1:T(8,128)}, f32[4,2,16,512]{3,2,1,0:T(8,128)}) async-done(((f32[4,2,16,512]{3,2,1,0:T(8,128)}, f32[4,1,16,1792]{3,2,0,1:T(8,128)}, f32[4,2,16,512]{3,2,1,0:T(8,128)}), (f32[4,2,16,512]{3,2,1,0:T(8,128)}, f32[4,1,16,1792]{3,2,0,1:T(8,128)}, f32[4,2,16,512]{3,2,1,0:T(8,128)})) %all-reduce.13.cloned.1.call-update) | async-done | bytes 983056 | tf_op jit(solution)/shard_map/psum | solution.py:58
  471.9 41.9 %all-reduce = (f32[4,2,16]{2,1,0:T(2,128)S(1)}, f32[4,1,16]{2,0,1:T(4,128)S(1)}, f32[4,2,16]{2,1,0:T(2,128)S(1)}) all-reduce(f32[4,2,16]{2,1,0:T(2,128)S(1)} %multiply_reduce_fusion.6, f32[4,1,16]{2,0,1:T(4,128)S(1)} %bitcast.31, f32[4,2,16]{2,1,0:T(2,128)S(1)} %multiply_reduce_fusion.8), channel_id=1, replica_groups=mesh['row_0'=16,'row_1'=4,'col'=8] {'row_0'}, use_global_device_ids=true, to_apply=%region_12.0 | all-reduce | flops 320 | bytes 2560 | tf_op jit(solution)/shard_map/psum | solution.py:26
  513.7 13.3 %all-reduce.4 = (f32[4,2,16]{2,1,0:T(2,128)S(1)}, f32[4,1,16]{2,0,1:T(4,128)S(1)}, f32[4,2,16]{2,1,0:T(2,128)S(1)}) all-reduce(f32[4,2,16]{2,1,0:T(2,128)S(1)} %get-tuple-element.6, f32[4,1,16]{2,0,1:T(4,128)S(1)} %get-tuple-element.7, f32[4,2,16]{2,1,0:T(2,128)S(1)} %get-tuple-element.8), channel_id=1, replica_groups=mesh['row_0'=16,'row_1'=4,'col'=8] {'row_1'}, use_global_device_ids=true, to_apply=%region_13.0 | all-reduce | flops 320 | bytes 2560 | tf_op jit(solution)/shard_map/psum | solution.py:26
  527.1 11.9 %all-reduce.17.cloned.1.call-done = (f32[4,2,16,512]{3,2,1,0:T(8,128)}, f32[4,1,16,1792]{3,2,0,1:T(8,128)}, f32[4,2,16,512]{3,2,1,0:T(8,128)}) async-done(((f32[4,2,16,512]{3,2,1,0:T(8,128)}, f32[4,1,16,1792]{3,2,0,1:T(8,128)}, f32[4,2,16,512]{3,2,1,0:T(8,128)}), (f32[4,2,16,512]{3,2,1,0:T(8,128)}, f32[4,1,16,1792]{3,2,0,1:T(8,128)}, f32[4,2,16,512]{3,2,1,0:T(8,128)})) %all-reduce.17.cloned.1.call-update) | async-done | bytes 983056 | tf_op jit(solution)/shard_map/psum | solution.py:58
  540.9 19.0 %all-to-all-start.7 = ((f32[8,4,1,16]{3,2,1,0:T(1,128)}), f32[8,4,1,16]{3,2,1,0:T(1,128)S(1)}, u32[]{:S(2)}, u32[]{:S(2)}) async-start(f32[8,4,1,16]{3,2,1,0:T(1,128)} %broadcast_in_dim.31), calls=%async_computation.7 | async-start | bytes 32768 | tf_op jit(solution)/shard_map/all_to_all | solution.py:14
  564.5 3.9 all-to-all-start.11
  573.0 3.9 all-to-all-start.3
  (129 shorter events, 82.1 us)
Async XLA Ops:
  7.2 22.3 %copy-start = (bf16[4,2,224,512]{3,2,1,0:T(8,128)(2,1)S(1)}, bf16[4,2,224,512]{3,2,1,0:T(8,128)(2,1)}, u32[]{:S(2)}) copy-start(bf16[4,2,224,512]{3,2,1,0:T(8,128)(2,1)} %param.6) | copy-start | bytes 5505028
  9.0 20.4 %copy-start.10 = (bf16[4,2,16,512]{3,2,1,0:T(8,128)(2,1)S(1)}, bf16[4,2,16,512]{3,2,1,0:T(8,128)(2,1)}, u32[]{:S(2)}) copy-start(bf16[4,2,16,512]{3,2,1,0:T(8,128)(2,1)} %param.9) | copy-start | bytes 393220
  9.9 15.4 %all-to-all-start.4 = ((f32[8,1,4096]{2,1,0:T(1,128)}), f32[8,1,4096]{2,1,0:T(1,128)S(1)}, u32[]{:S(2)}, u32[]{:S(2)}) async-start(f32[8,1,4096]{2,1,0:T(1,128)} %reshape.197), calls=%async_computation.4 | async-start | bytes 262144 | tf_op jit(solution)/shard_map/all_to_all | solution.py:14
  25.2 10.7 %all-to-all-start.8 = ((f32[8,1,8192]{2,1,0:T(1,128)}), f32[8,1,8192]{2,1,0:T(1,128)S(1)}, u32[]{:S(2)}, u32[]{:S(2)}) async-start(f32[8,1,8192]{2,1,0:T(1,128)} %reshape.201), calls=%async_computation.8 | async-start | bytes 524288 | tf_op jit(solution)/shard_map/all_to_all | solution.py:14
  30.7 18.8 %copy-start.1 = (bf16[4,64,1792]{2,1,0:T(8,128)(2,1)S(1)}, bf16[4,64,1792]{2,1,0:T(8,128)(2,1)}, u32[]{:S(2)}) copy-start(bf16[4,64,1792]{2,1,0:T(8,128)(2,1)} %param.7) | copy-start | bytes 2752516
  38.1 20.2 %all-to-all-start = ((f32[8,4,2,16,224]{4,3,2,1,0:T(8,128)}), f32[8,4,2,16,224]{4,3,2,1,0:T(8,128)}, u32[]{:S(2)}, u32[]{:S(2)}) async-start(f32[8,4,2,16,224]{4,3,2,1,0:T(8,128)} %broadcast_in_dim.24), calls=%async_computation | async-start | bytes 2097152 | tf_op jit(solution)/shard_map/all_to_all | solution.py:14
  43.2 146.5 %all-reduce.15.cloned.1.call-start = ((), (), s32[]{:S(2)}) async-start(), calls=%async_computation.13 | async-start | bytes 1966080 | tf_op jit(solution)/shard_map/psum | solution.py:58
  59.7 130.1 %copy-start.8 = (f32[4,16,64]{2,1,0:T(8,128)S(1)}, f32[4,16,64]{2,1,0:T(8,128)}, u32[]{:S(2)}) copy-start(f32[4,16,64]{2,1,0:T(8,128)} %reduce_sum.228) | copy-start | bytes 49156
  60.7 196.6 %all-reduce.19.cloned.1.call-start = ((), (), s32[]{:S(2)}) async-start(), calls=%async_computation.15 | async-start | bytes 1966080 | tf_op jit(solution)/shard_map/psum | solution.py:58
  259.2 23.5 %all-to-all-start.5 = ((f32[8,4,1,16]{3,2,1,0:T(1,128)}), f32[8,4,1,16]{3,2,1,0:T(1,128)S(1)}, u32[]{:S(2)}, u32[]{:S(2)}) async-start(f32[8,4,1,16]{3,2,1,0:T(1,128)} %broadcast_in_dim.29), calls=%async_computation.5 | async-start | bytes 32768 | tf_op jit(solution)/shard_map/all_to_all | solution.py:14
  282.7 8.5 %all-to-all-start.9 = ((f32[8,1,128]{2,1,0:T(1,128)}), f32[8,1,128]{2,1,0:T(1,128)S(1)}, u32[]{:S(2)}, u32[]{:S(2)}) async-start(f32[8,1,128]{2,1,0:T(1,128)} %reshape.203), calls=%async_computation.9 | async-start | bytes 8192 | tf_op jit(solution)/shard_map/all_to_all | solution.py:14
  288.8 29.1 %copy-start.3 = (f32[4,2,16,512]{3,2,1,0:T(8,128)S(1)}, f32[4,2,16,512]{3,2,1,0:T(8,128)}, u32[]{:S(2)}) copy-start(f32[4,2,16,512]{3,2,1,0:T(8,128)} %get-tuple-element.27) | copy-start | bytes 786436
  291.7 11.3 %all-to-all-start.1 = ((f32[8,1,128]{2,1,0:T(1,128)}), f32[8,1,128]{2,1,0:T(1,128)S(1)}, u32[]{:S(2)}, u32[]{:S(2)}) async-start(f32[8,1,128]{2,1,0:T(1,128)} %reshape.193), calls=%async_computation.1 | async-start | bytes 8192 | tf_op jit(solution)/shard_map/all_to_all | solution.py:14
  303.0 10.2 %all-to-all-start.6 = ((f32[8,1,4096]{2,1,0:T(1,128)}), f32[8,1,4096]{2,1,0:T(1,128)}, u32[]{:S(2)}, u32[]{:S(2)}) async-start(f32[8,1,4096]{2,1,0:T(1,128)} %reshape.199), calls=%async_computation.6 | async-start | bytes 262144 | tf_op jit(solution)/shard_map/all_to_all | solution.py:14
  313.2 11.4 %all-to-all-start.10 = ((f32[8,1,8192]{2,1,0:T(1,128)}), f32[8,1,8192]{2,1,0:T(1,128)}, u32[]{:S(2)}, u32[]{:S(2)}) async-start(f32[8,1,8192]{2,1,0:T(1,128)} %reshape.205), calls=%async_computation.10 | async-start | bytes 524288 | tf_op jit(solution)/shard_map/all_to_all | solution.py:14
  326.6 20.2 %all-to-all-start.2 = ((f32[8,4,2,16,224]{4,3,2,1,0:T(8,128)}), f32[8,4,2,16,224]{4,3,2,1,0:T(8,128)}, u32[]{:S(2)}, u32[]{:S(2)}) async-start(f32[8,4,2,16,224]{4,3,2,1,0:T(8,128)} %broadcast_in_dim.26), calls=%async_computation.2 | async-start | bytes 2097152 | tf_op jit(solution)/shard_map/all_to_all | solution.py:14
  331.8 139.8 %all-reduce.13.cloned.1.call-start = ((), (), s32[]{:S(2)}) async-start(), calls=%async_computation.12 | async-start | bytes 1966080 | tf_op jit(solution)/shard_map/psum | solution.py:58
  348.2 123.4 %copy-start.9 = (f32[4,16,64]{2,1,0:T(8,128)S(1)}, f32[4,16,64]{2,1,0:T(8,128)}, u32[]{:S(2)}) copy-start(f32[4,16,64]{2,1,0:T(8,128)} %reduce_sum.233) | copy-start | bytes 49156
  349.3 189.7 %all-reduce.17.cloned.1.call-start = ((), (), s32[]{:S(2)}) async-start(), calls=%async_computation.14 | async-start | bytes 1966080 | tf_op jit(solution)/shard_map/psum | solution.py:58
  539.0 39.2 %copy-start.6 = (f32[4,2,16,512]{3,2,1,0:T(8,128)S(1)}, f32[4,2,16,512]{3,2,1,0:T(8,128)}, u32[]{:S(2)}) copy-start(f32[4,2,16,512]{3,2,1,0:T(8,128)} %get-tuple-element.26) | copy-start | bytes 786436
  539.0 43.8 %copy-start.5 = (f32[4,2,16,512]{3,2,1,0:T(8,128)S(1)}, f32[4,2,16,512]{3,2,1,0:T(8,128)}, u32[]{:S(2)}) copy-start(f32[4,2,16,512]{3,2,1,0:T(8,128)} %get-tuple-element.24) | copy-start | bytes 786436
  540.9 23.6 %all-to-all-start.7 = ((f32[8,4,1,16]{3,2,1,0:T(1,128)}), f32[8,4,1,16]{3,2,1,0:T(1,128)S(1)}, u32[]{:S(2)}, u32[]{:S(2)}) async-start(f32[8,4,1,16]{3,2,1,0:T(1,128)} %broadcast_in_dim.31), calls=%async_computation.7 | async-start | bytes 32768 | tf_op jit(solution)/shard_map/all_to_all | solution.py:14
  564.5 8.5 %all-to-all-start.11 = ((f32[8,1,128]{2,1,0:T(1,128)}), f32[8,1,128]{2,1,0:T(1,128)S(1)}, u32[]{:S(2)}, u32[]{:S(2)}) async-start(f32[8,1,128]{2,1,0:T(1,128)} %reshape.207), calls=%async_computation.11 | async-start | bytes 8192 | tf_op jit(solution)/shard_map/all_to_all | solution.py:14
  573.0 8.5 %all-to-all-start.3 = ((f32[8,1,128]{2,1,0:T(1,128)}), f32[8,1,128]{2,1,0:T(1,128)S(1)}, u32[]{:S(2)}, u32[]{:S(2)}) async-start(f32[8,1,128]{2,1,0:T(1,128)} %reshape.195), calls=%async_computation.3 | async-start | bytes 8192 | tf_op jit(solution)/shard_map/all_to_all | solution.py:14
  (5 other events, 42.3 us)
Sparse Core Ops, SparseCore 0:
  60.9 128.8 all-reduce.14
  192.3 65.0 all-reduce.18
  349.4 122.0 all-reduce.12
  473.9 65.0 all-reduce.16
